TPU v7x, 32 devices: a whole 2x2x4 slice. The times are simulated.
32 devices in a mesh: dp: 2 (over x), expert: 4 (over z), mp: 4 (over y, core).
Axes of the slice: x: 2, y: 2, z: 4, core: 2. Of those that a mesh axis runs over, the one named last changes fastest.
Arguments:
- tokens: bfloat16 [128, 4096], P(('dp', 'expert', 'mp')), may hold values from -6 to 6
- probes: bfloat16 [2, 128, 4096], P(None, ('dp', 'expert', 'mp')), may hold values from -6 to 6
- cotangent: bfloat16 [128, 4096], P(('dp', 'expert', 'mp')), may hold values from -0.119628906 to 0.119628906
- expert_ids: int32 [128, 2], P(('dp', 'expert', 'mp')), may hold values from 0 to 3, all different within a row; in each aligned block of 4 rows (0 to 3, 4 to 7, ...) at most 4 rows name the same one
- combine: float32 [128, 2], P(('dp', 'expert', 'mp')), may hold values from 0.2 to 1
- w_gate: bfloat16 [4, 4096, 14336], P('expert', None, ('dp', 'mp')), may hold values from -0.09375 to 0.09375
- w_up: bfloat16 [4, 4096, 14336], P('expert', None, ('dp', 'mp')), may hold values from -0.09375 to 0.09375
- w_down: bfloat16 [4, 14336, 4096], P('expert', ('dp', 'mp')), may hold values from -0.046875 to 0.046875
Outputs:
- quad: float32 [2, 128], P(None, ('dp', 'expert', 'mp'))
Inputs may be any that keep to these rules, and one draw needn't show every extreme that they name: `expert_ids`: each token names 2 different experts. In each aligned block of 4 tokens (the tokens of one device) no expert is named by more than 4 of them, and some block reaches 4.
All inputs are finite; a program needn't handle non-finite values.
Results may differ from a plain program's by a relative error of at most 0.003.
Values may be sent and summed in bfloat16 or wider, within the bound.
No kernel may reach another device: no remote copies, remote signals or barrier semaphores. Data moves between devices by JAX's collectives and lax.ppermute only.
A program may use at most 128 MiB of HBM per device.

v0:
```python
import jax
import jax.numpy as jnp
from jax import lax
from jax.sharding import PartitionSpec as P


def silu_slopes(preact):
    squash = jax.nn.sigmoid(preact)
    first_slope = squash * (1.0 + preact * (1.0 - squash))
    second_slope = squash * (1.0 - squash) * (2.0 + preact * (1.0 - 2.0 * squash))
    return (first_slope, second_slope)


def on_device(tokens, probes, cotangent, expert_ids, combine, w_gate, w_up, w_down):
    tok_dev, model_width = tokens.shape
    probe_count = probes.shape[0]
    top_count = expert_ids.shape[1]
    experts = lax.axis_size("expert") * w_gate.shape[0]
    capacity = 2 * max(1, tok_dev * top_count // experts)
    routed = tok_dev * top_count
    flat_ids = expert_ids.reshape(routed)
    positions = jnp.arange(routed, dtype=jnp.int32)
    same_expert = flat_ids[:, None] == flat_ids[None, :]
    before = positions[None, :] < positions[:, None]
    slot_index = jnp.sum((same_expert & before).astype(jnp.int32), axis=1)
    expert_hot = flat_ids[:, None] == jnp.arange(experts, dtype=jnp.int32)[None, :]
    slot_hot = slot_index[:, None] == jnp.arange(capacity, dtype=jnp.int32)[None, :]
    placing = (expert_hot[:, :, None] & slot_hot[:, None, :]).reshape(routed, experts * capacity)
    scaled = (
        combine.reshape(routed, 1) * jnp.repeat(cotangent.astype(jnp.float32), top_count, axis=0)
    ).astype(jnp.bfloat16)
    stacked = jnp.repeat(jnp.concatenate([tokens[None], probes], axis=0), top_count, axis=1)
    stacked = jnp.concatenate([stacked, scaled[None]], axis=0)
    outgoing = jnp.einsum(
        "nk,rnd->rkd", placing.astype(jnp.bfloat16), stacked, preferred_element_type=jnp.float32
    ).astype(jnp.bfloat16)
    outgoing = outgoing.reshape(probe_count + 2, experts, capacity, model_width)
    arrived = lax.all_to_all(outgoing, "expert", split_axis=1, concat_axis=1, tiled=True)
    arrived = arrived.reshape(probe_count + 2, experts * capacity, model_width)
    gate_local = w_gate[0]
    up_local = w_up[0]
    down_local = w_down[0]
    block_rows = lax.all_gather(arrived, ("dp", "mp"), axis=1, tiled=True)
    row_count = block_rows.shape[1]
    base_rows = block_rows[0]
    tangent = block_rows[1 : probe_count + 1].reshape(probe_count * row_count, model_width)
    readout_rows = block_rows[probe_count + 1]
    gate_pre = jnp.dot(base_rows, gate_local, preferred_element_type=jnp.float32)
    up_pre = jnp.dot(base_rows, up_local, preferred_element_type=jnp.float32)
    readout = lax.dot_general(
        readout_rows, down_local, (((1,), (1,)), ((), ())), preferred_element_type=jnp.float32
    )
    gate_tan = jnp.dot(tangent, gate_local, preferred_element_type=jnp.float32).reshape(
        probe_count, row_count, -1
    )
    up_tan = jnp.dot(tangent, up_local, preferred_element_type=jnp.float32).reshape(
        probe_count, row_count, -1
    )
    first_slope, second_slope = silu_slopes(gate_pre)
    curved = second_slope * gate_tan * gate_tan * up_pre + 2.0 * first_slope * gate_tan * up_tan
    partial_quad = jnp.sum(curved * readout, axis=2)
    spread = partial_quad.reshape(probe_count, -1, experts, capacity)
    swapped = lax.all_to_all(spread, "expert", split_axis=2, concat_axis=2, tiled=True)
    returned_table = lax.psum_scatter(swapped, ("dp", "mp"), scatter_dimension=1, tiled=True)
    returned_table = returned_table.reshape(probe_count, experts * capacity)
    per_choice = jnp.dot(
        returned_table, placing.astype(jnp.float32).T, precision=lax.Precision.HIGHEST
    )
    return jnp.sum(per_choice.reshape(probe_count, tok_dev, top_count), axis=2)


def solution(mesh):
    in_specs = (
        P(("dp", "expert", "mp"), None),
        P(None, ("dp", "expert", "mp"), None),
        P(("dp", "expert", "mp"), None),
        P(("dp", "expert", "mp"), None),
        P(("dp", "expert", "mp"), None),
        P("expert", None, ("dp", "mp")),
        P("expert", None, ("dp", "mp")),
        P("expert", ("dp", "mp"), None),
    )
    out_specs = P(None, ("dp", "expert", "mp"))
    return jax.shard_map(
        on_device, mesh=mesh, in_specs=in_specs, out_specs=out_specs, check_vma=False
    )
```

profile of v0, /device:TPU:0, one launch (start us, length us, event | category | flops | bytes accessed | tf_op | source)
XLA Modules:
  0.0 151.4 jit_solution(9629628665399387584)
XLA Ops:
  6.5 0.8 copy.29
  7.4 0.2 convert_reduce_fusion
  7.9 0.8 copy.28
  8.7 0.9 pad_maximum_fusion
  9.8 0.8 broadcast_in_dim.8
  10.8 0.3 fusion.10
  11.1 0.2 reshape.134
  11.3 0.2 copy.32
  11.5 20.6 %all_to_all.10 = bf16[4,4,4,4096]{3,2,0,1:T(4,128)(2,1)S(1)} all-to-all(bf16[4,4,4,4096]{3,2,0,1:T(4,128)(2,1)S(1)} %copy.32), channel_id=1, replica_groups=mesh['dp'=2,'expert'=4,'mp'=4] {'expert'}, dimensions={1} | all-to-all | bytes 1048576 | tf_op jit(solution)/shard_map/all_to_all | solution.py:38
  32.2 0.2 copy.33
  32.4 0.9 reshape.135
  33.3 35.8 %all-gather.2.cloned.1.call-done = bf16[4,128,4096]{2,1,0:T(8,128)(2,1)} async-done(((bf16[4,16,4096]{2,1,0:T(8,128)(2,1)}), bf16[4,128,4096]{2,1,0:T(8,128)(2,1)}) %all-gather.2.cloned.1.call-update) | async-done | bytes 4194320 | tf_op jit(solution)/shard_map/all_gather | solution.py:43
  69.2 8.7 %fusion.6 = f32[2,128,1792]{2,1,0:T(8,128)S(1)} fusion(bf16[4,128,4096]{2,1,0:T(8,128)(2,1)} %all-gather.2.cloned.1.call-done, bf16[1,4096,1792]{2,1,0:T(8,128)(2,1)} %param.13), kind=kOutput, calls=%fused_computation.6 | convolution fusion | flops 3758096384 | bytes 20709376 | tf_op jit(solution)/shard_map/dot_general | solution.py:53
  77.9 9.5 %fusion.24 = (f32[128,1792]{1,0:T(8,128)S(1)}, f32[128,1792]{1,0:T(8,128)}) fusion(bf16[1,4096,1792]{2,1,0:T(8,128)(2,1)} %param.13, bf16[4,128,4096]{2,1,0:T(8,128)(2,1)S(1)} %copy-done), kind=kOutput, calls=%fused_computation.23 | convolution fusion | flops 1882259456 | bytes 17563648 | tf_op jit(solution)/shard_map/dot_general | solution.py:48
  87.5 2.2 %fusion.4 = f32[128,1792]{1,0:T(8,128)S(1)} fusion(bf16[1,4096,1792]{2,1,0:T(8,128)(2,1)S(1)} %bitcast.48, bf16[4,128,4096]{2,1,0:T(8,128)(2,1)S(1)} %copy-done), kind=kOutput, calls=%fused_computation.4 | convolution fusion | flops 1879048192 | bytes 16646144 | tf_op jit(solution)/shard_map/dot_general | solution.py:49
  89.6 10.1 %fusion = f32[128,1792]{1,0:T(8,128)S(1)} fusion(bf16[1,1792,4096]{2,1,0:T(8,128)(2,1)} %param.15, bf16[4,128,4096]{2,1,0:T(8,128)(2,1)S(1)} %copy-done), kind=kOutput, calls=%fused_computation | convolution fusion | flops 1879048192 | bytes 16646144 | tf_op jit(solution)/shard_map/dot_general | solution.py:50
  99.8 9.7 %fusion.21 = f32[2,128]{1,0:T(2,128)S(1)} fusion(bf16[4,128,4096]{2,1,0:T(8,128)(2,1)S(1)} %copy-done, bf16[1,4096,1792]{2,1,0:T(8,128)(2,1)} %param.14, f32[2,128,1792]{2,1,0:T(8,128)S(1)} %fusion.6, f32[128,1792]{1,0:T(8,128)S(1)} %fusion, f32[128,1792]{1,0:T(8,128)} %get-tuple-element.6, f32[128,1792]{1,0:T(8,128)S(1)} %fusion.4, ...), kind=kOutput, calls=%fused_computation.17 | convolution fusion | flops 3761766144 | bytes 24380416 | tf_op jit(solution)/shard_map/dot_general | solution.py:56
  109.6 0.7 copy.34
  110.3 4.6 %all-to-all-start.1 = ((f32[2,8,4,4]{1,3,0,2:T(4,128)}), f32[2,8,4,4]{1,3,0,2:T(4,128)S(1)}, u32[]{:S(2)}, u32[]{:S(2)}) async-start(f32[2,8,4,4]{1,3,0,2:T(4,128)} %copy.34), calls=%async_computation.1 | async-start | bytes 32768 | tf_op jit(solution)/shard_map/all_to_all | solution.py:63
  115.0 0.6 dynamic-slice
  115.6 4.9 %all-to-all-done.1 = f32[2,8,4,4]{1,3,0,2:T(4,128)S(1)} async-done(((f32[2,8,4,4]{1,3,0,2:T(4,128)}), f32[2,8,4,4]{1,3,0,2:T(4,128)S(1)}, u32[]{:S(2)}, u32[]{:S(2)}) %all-to-all-start.1) | async-done | bytes 1056 | tf_op jit(solution)/shard_map/all_to_all | solution.py:63
  120.7 22.3 %all-reduce = f32[2,8,4,4]{3,2,1,0:T(4,128)S(1)} all-reduce(f32[2,8,4,4]{3,2,1,0:T(4,128)S(1)} %copy.35), channel_id=2, replica_groups=mesh['dp'=2,'expert'=4,'mp'=4] {'dp','mp'}, use_global_device_ids=true, to_apply=%region_2.0.clone | all-reduce | flops 256 | bytes 2048
  143.0 0.6 constant_dynamic-slice_fusion
  143.8 0.8 convolution_reduce_fusion
  (28 shorter events, 1.3 us)
Async XLA Ops:
  6.5 62.6 %all-gather.2.cloned.1.call-start = ((), (), s32[]{:S(2)}) async-start(), calls=%async_computation.2 | async-start | bytes 4718592 | tf_op jit(solution)/shard_map/all_gather | solution.py:43
  69.2 8.8 %copy-start = (bf16[4,128,4096]{2,1,0:T(8,128)(2,1)S(1)}, bf16[4,128,4096]{2,1,0:T(8,128)(2,1)}, u32[]{:S(2)}) copy-start(bf16[4,128,4096]{2,1,0:T(8,128)(2,1)} %all-gather.2.cloned.1.call-done) | copy-start | bytes 12582916
  69.2 18.3 %slice-start = ((s8[14680064]{0:T(1024)(128)(4,1)}), s8[4194304]{0:T(1024)(128)(4,1)S(1)}, s32[]{:S(2)}) async-start(s8[14680064]{0:T(1024)(128)(4,1)} %bitcast.47), calls=%async_computation.3 | async-start | bytes 8388608
  69.2 18.3 %slice-start.1 = ((s8[14680064]{0:T(1024)(128)(4,1)}), s8[4194304]{0:T(1024)(128)(4,1)S(1)}, s32[]{:S(2)}) async-start(s8[14680064]{0:T(1024)(128)(4,1)} %bitcast.47), calls=%async_computation.4 | async-start | bytes 8388608
  69.2 18.3 %slice-start.2 = ((s8[14680064]{0:T(1024)(128)(4,1)}), s8[4194304]{0:T(1024)(128)(4,1)S(1)}, s32[]{:S(2)}) async-start(s8[14680064]{0:T(1024)(128)(4,1)} %bitcast.47), calls=%async_computation.5 | async-start | bytes 8388608
  77.9 9.5 %slice-start.3 = ((s8[14680064]{0:T(1024)(128)(4,1)}), s8[2097152]{0:T(1024)(128)(4,1)S(1)}, s32[]{:S(2)}) async-start(s8[14680064]{0:T(1024)(128)(4,1)} %bitcast.47), calls=%async_computation.6 | async-start | bytes 4194304
  99.8 15.2 %copy-start.1 = (u32[32]{0:T(128)S(1)}, u32[32]{0:T(128)}, u32[]{:S(2)}) copy-start(u32[32]{0:T(128)} %constant.18) | copy-start | bytes 388
  110.3 10.2 %all-to-all-start.1 = ((f32[2,8,4,4]{1,3,0,2:T(4,128)}), f32[2,8,4,4]{1,3,0,2:T(4,128)S(1)}, u32[]{:S(2)}, u32[]{:S(2)}) async-start(f32[2,8,4,4]{1,3,0,2:T(4,128)} %copy.34), calls=%async_computation.1 | async-start | bytes 32768 | tf_op jit(solution)/shard_map/all_to_all | solution.py:63
Sparse Core Ops, SparseCore 0:
  33.4 35.6 all-gather.1
where the time goes:
time: 152 us; the launch traced here: 151 us
  blocking collectives  43 us (28%)
  matrix products  41.3 us (27%)
  waiting for transfers between devices  40.8 us (27%)
  between operations  13.5 us (9%)
  local copies, waits for them, and re-layouts  6.85 us (5%)
  starting transfers between devices  4.6 us (3%)
    all_gather x1, waiting for transfers between devices, on_device(): block_rows = lax.all_gather(arrived, ('dp', 'mp'), axis=1, tiled=True)  35.8 us
    unnamed x1, blocking collectives  22.3 us
    all_to_all x1, blocking collectives, on_device(): lax.all_to_all(outgoing, 'expert', split_axis=1, concat_axis=1, tiled=True)  20.6 us
    dot_general x1, matrix products, on_device(): lax.dot_general(readout_rows, down_local, (((1,), (1,)), ((), ())), prefe...  10.1 us
    dot_general x1, matrix products, on_device(): jnp.dot(tangent, up_local, preferred_element_type=jnp.float32)  9.69 us
    dot_general x1, matrix products, on_device(): jnp.dot(base_rows, gate_local, preferred_element_type=jnp.float32)  9.49 us
    dot_general x1, matrix products, on_device(): jnp.dot(tangent, gate_local, preferred_element_type=jnp.float32)  8.75 us
    all_to_all x1, waiting for transfers between devices, on_device(): lax.all_to_all(spread, 'expert', split_axis=2, concat_axis=2, tiled=True)  4.94 us
  transfers between devices with their start and end apart: 2, of which 2 were waited for; matrix products, arithmetic and copies ran while one was open for 0% of the time, Pallas kernels for 0%

commit v1 on v0

--- a/solution.py
+++ b/solution.py
@@ -35,7 +35,12 @@
         "nk,rnd->rkd", placing.astype(jnp.bfloat16), stacked, preferred_element_type=jnp.float32
     ).astype(jnp.bfloat16)
     outgoing = outgoing.reshape(probe_count + 2, experts, capacity, model_width)
-    arrived = lax.all_to_all(outgoing, "expert", split_axis=1, concat_axis=1, tiled=True)
+    arrived = jnp.concatenate(
+        lax.all_to_all(
+            jnp.stack(jnp.split(outgoing, lax.axis_size("expert"), axis=1)), "expert", 0, 0
+        ),
+        axis=1,
+    )
     arrived = arrived.reshape(probe_count + 2, experts * capacity, model_width)
     gate_local = w_gate[0]
     up_local = w_up[0]

time: 152 us -> 152 us (level)
  no operation moved by 1% of the time
where the time goes in v1:
time: 152 us
  blocking collectives  43 us (28%)
  matrix products  41.4 us (27%)
  waiting for transfers between devices  40.8 us (27%)
  between operations  13.6 us (9%)
  local copies, waits for them, and re-layouts  6.85 us (5%)
  starting transfers between devices  4.6 us (3%)
  other arithmetic  1.8 us (1%)
    all_gather x1, waiting for transfers between devices, on_device(): block_rows = lax.all_gather(arrived, ('dp', 'mp'), axis=1, tiled=True)  35.8 us
    unnamed x1, blocking collectives  22.3 us
    all_to_all x1, blocking collectives, on_device(): lax.all_to_all(jnp.stack(jnp.split(outgoing, lax.axis_size('expert'), axi...  20.6 us
    dot_general x1, matrix products, on_device(): lax.dot_general(readout_rows, down_local, (((1,), (1,)), ((), ())), prefe...  10.1 us
    dot_general x1, matrix products, on_device(): jnp.dot(tangent, up_local, preferred_element_type=jnp.float32)  9.77 us
    dot_general x1, matrix products, on_device(): jnp.dot(base_rows, gate_local, preferred_element_type=jnp.float32)  9.51 us
    dot_general x1, matrix products, on_device(): jnp.dot(tangent, gate_local, preferred_element_type=jnp.float32)  8.75 us
    all_to_all x1, waiting for transfers between devices, on_device(): lax.all_to_all(spread, 'expert', split_axis=2, concat_axis=2, tiled=True)  4.94 us
  transfers between devices with their start and end apart: 2, of which 2 were waited for; matrix products, arithmetic and copies ran while one was open for 0% of the time, Pallas kernels for 0%

profile of v1, /device:TPU:0, one launch (start us, length us, event | category | flops | bytes accessed | tf_op | source)
XLA Modules:
  0.0 152.0 jit_solution(13193229490154965615)
XLA Ops:
  6.5 0.8 copy.39
  7.9 0.8 copy.38
  8.7 0.9 pad_maximum_fusion.1
  9.8 0.8 broadcast_in_dim.8
  10.8 0.3 fusion.10
  11.1 0.2 reshape.134
  11.3 0.2 slice_bitcast_fusion.8
  11.5 0.5 pad_maximum_fusion
  12.0 20.6 %all_to_all.10 = bf16[4,4,1,4,4096]{4,3,1,2,0:T(4,128)(2,1)S(1)} all-to-all(bf16[4,4,1,4,4096]{4,3,1,2,0:T(4,128)(2,1)S(1)} %pad_maximum_fusion), channel_id=1, replica_groups=mesh['dp'=2,'expert'=4,'mp'=4] {'expert'}, dimensions={0} | all-to-all | bytes 1048576 | tf_op jit(solution)/shard_map/all_to_all | solution.py:39
  32.6 0.2 copy.45
  32.8 0.9 reshape_reshape.3
  33.8 35.8 %all-gather.2.cloned.1.call-done = bf16[4,128,4096]{2,1,0:T(8,128)(2,1)} async-done(((bf16[4,16,4096]{2,1,0:T(8,128)(2,1)}), bf16[4,128,4096]{2,1,0:T(8,128)(2,1)}) %all-gather.2.cloned.1.call-update) | async-done | bytes 4194320 | tf_op jit(solution)/shard_map/all_gather | solution.py:48
  69.6 8.8 %fusion.6 = f32[2,128,1792]{2,1,0:T(8,128)S(1)} fusion(bf16[4,128,4096]{2,1,0:T(8,128)(2,1)} %all-gather.2.cloned.1.call-done, bf16[1,4096,1792]{2,1,0:T(8,128)(2,1)} %param.13), kind=kOutput, calls=%fused_computation.6 | convolution fusion | flops 3758096384 | bytes 20709376 | tf_op jit(solution)/shard_map/dot_general | solution.py:58
  78.4 9.5 %fusion.24 = (f32[128,1792]{1,0:T(8,128)S(1)}, f32[128,1792]{1,0:T(8,128)}) fusion(bf16[1,4096,1792]{2,1,0:T(8,128)(2,1)} %param.13, bf16[4,128,4096]{2,1,0:T(8,128)(2,1)S(1)} %copy-done), kind=kOutput, calls=%fused_computation.23 | convolution fusion | flops 1882259456 | bytes 17563648 | tf_op jit(solution)/shard_map/dot_general | solution.py:53
  88.0 2.2 %fusion.4 = f32[128,1792]{1,0:T(8,128)S(1)} fusion(bf16[1,4096,1792]{2,1,0:T(8,128)(2,1)S(1)} %bitcast.65, bf16[4,128,4096]{2,1,0:T(8,128)(2,1)S(1)} %copy-done), kind=kOutput, calls=%fused_computation.4 | convolution fusion | flops 1879048192 | bytes 16646144 | tf_op jit(solution)/shard_map/dot_general | solution.py:54
  90.2 10.1 %fusion = f32[128,1792]{1,0:T(8,128)S(1)} fusion(bf16[1,1792,4096]{2,1,0:T(8,128)(2,1)} %param.15, bf16[4,128,4096]{2,1,0:T(8,128)(2,1)S(1)} %copy-done), kind=kOutput, calls=%fused_computation | convolution fusion | flops 1879048192 | bytes 16646144 | tf_op jit(solution)/shard_map/dot_general | solution.py:55
  100.4 9.8 %fusion.21 = f32[2,128]{1,0:T(2,128)S(1)} fusion(bf16[4,128,4096]{2,1,0:T(8,128)(2,1)S(1)} %copy-done, bf16[1,4096,1792]{2,1,0:T(8,128)(2,1)} %param.14, f32[2,128,1792]{2,1,0:T(8,128)S(1)} %fusion.6, f32[128,1792]{1,0:T(8,128)S(1)} %fusion, f32[128,1792]{1,0:T(8,128)} %get-tuple-element.6, f32[128,1792]{1,0:T(8,128)S(1)} %fusion.4, ...), kind=kOutput, calls=%fused_computation.17 | convolution fusion | flops 3761766144 | bytes 24380416 | tf_op jit(solution)/shard_map/dot_general | solution.py:61
  110.2 0.7 copy.46
  111.0 4.6 %all-to-all-start.1 = ((f32[2,8,4,4]{1,3,0,2:T(4,128)}), f32[2,8,4,4]{1,3,0,2:T(4,128)S(1)}, u32[]{:S(2)}, u32[]{:S(2)}) async-start(f32[2,8,4,4]{1,3,0,2:T(4,128)} %copy.46), calls=%async_computation.1 | async-start | bytes 32768 | tf_op jit(solution)/shard_map/all_to_all | solution.py:68
  115.7 0.6 dynamic-slice
  116.3 4.9 %all-to-all-done.1 = f32[2,8,4,4]{1,3,0,2:T(4,128)S(1)} async-done(((f32[2,8,4,4]{1,3,0,2:T(4,128)}), f32[2,8,4,4]{1,3,0,2:T(4,128)S(1)}, u32[]{:S(2)}, u32[]{:S(2)}) %all-to-all-start.1) | async-done | bytes 1056 | tf_op jit(solution)/shard_map/all_to_all | solution.py:68
  121.3 22.3 %all-reduce = f32[2,8,4,4]{3,2,1,0:T(4,128)S(1)} all-reduce(f32[2,8,4,4]{3,2,1,0:T(4,128)S(1)} %copy.47), channel_id=2, replica_groups=mesh['dp'=2,'expert'=4,'mp'=4] {'dp','mp'}, use_global_device_ids=true, to_apply=%region_2.0.clone | all-reduce | flops 256 | bytes 2048
  143.7 0.6 constant_dynamic-slice_fusion
  144.4 0.8 convolution_reduce_fusion
  (29 shorter events, 1.5 us)
Async XLA Ops:
  6.5 63.1 %all-gather.2.cloned.1.call-start = ((), (), s32[]{:S(2)}) async-start(), calls=%async_computation.2 | async-start | bytes 4718592 | tf_op jit(solution)/shard_map/all_gather | solution.py:48
  69.6 8.8 %copy-start = (bf16[4,128,4096]{2,1,0:T(8,128)(2,1)S(1)}, bf16[4,128,4096]{2,1,0:T(8,128)(2,1)}, u32[]{:S(2)}) copy-start(bf16[4,128,4096]{2,1,0:T(8,128)(2,1)} %all-gather.2.cloned.1.call-done) | copy-start | bytes 12582916
  69.6 18.3 %slice-start = ((s8[14680064]{0:T(1024)(128)(4,1)}), s8[4194304]{0:T(1024)(128)(4,1)S(1)}, s32[]{:S(2)}) async-start(s8[14680064]{0:T(1024)(128)(4,1)} %bitcast.64), calls=%async_computation.3 | async-start | bytes 8388608
  69.6 18.3 %slice-start.1 = ((s8[14680064]{0:T(1024)(128)(4,1)}), s8[4194304]{0:T(1024)(128)(4,1)S(1)}, s32[]{:S(2)}) async-start(s8[14680064]{0:T(1024)(128)(4,1)} %bitcast.64), calls=%async_computation.4 | async-start | bytes 8388608
  69.6 18.3 %slice-start.2 = ((s8[14680064]{0:T(1024)(128)(4,1)}), s8[4194304]{0:T(1024)(128)(4,1)S(1)}, s32[]{:S(2)}) async-start(s8[14680064]{0:T(1024)(128)(4,1)} %bitcast.64), calls=%async_computation.5 | async-start | bytes 8388608
  78.4 9.5 %slice-start.3 = ((s8[14680064]{0:T(1024)(128)(4,1)}), s8[2097152]{0:T(1024)(128)(4,1)S(1)}, s32[]{:S(2)}) async-start(s8[14680064]{0:T(1024)(128)(4,1)} %bitcast.64), calls=%async_computation.6 | async-start | bytes 4194304
  100.3 15.3 %copy-start.1 = (u32[32]{0:T(128)S(1)}, u32[32]{0:T(128)}, u32[]{:S(2)}) copy-start(u32[32]{0:T(128)} %constant.18) | copy-start | bytes 388
  111.0 10.2 %all-to-all-start.1 = ((f32[2,8,4,4]{1,3,0,2:T(4,128)}), f32[2,8,4,4]{1,3,0,2:T(4,128)S(1)}, u32[]{:S(2)}, u32[]{:S(2)}) async-start(f32[2,8,4,4]{1,3,0,2:T(4,128)} %copy.46), calls=%async_computation.1 | async-start | bytes 32768 | tf_op jit(solution)/shard_map/all_to_all | solution.py:68
Sparse Core Ops, SparseCore 0:
  33.9 35.6 all-gather.1
